TPU v7x, 256 devices: a whole 4x4x8 slice. The times are simulated.
256 devices in a mesh: fsdp: 16 (over z, core), tp: 16 (over y, x).
Axes of the slice: x: 4, y: 4, z: 8, core: 2. Of those that a mesh axis runs over, the one named last changes fastest.
Arguments:
- w_gate: bfloat16 [4096, 11008], P('fsdp', 'tp'), may hold values from -0.09375 to 0.09375
- low_gate: bfloat16 [4096, 16], P('fsdp'), may hold values from -0.09375 to 0.09375
- high_gate: bfloat16 [16, 11008], P(None, 'tp'), may hold values from -1.5 to 1.5
- w_up: bfloat16 [4096, 11008], P('fsdp', 'tp'), may hold values from -0.09375 to 0.09375
- low_up: bfloat16 [4096, 16], P('fsdp'), may hold values from -0.09375 to 0.09375
- high_up: bfloat16 [16, 11008], P(None, 'tp'), may hold values from -1.5 to 1.5
- w_down: bfloat16 [11008, 4096], P('tp', 'fsdp'), may hold values from -0.0546875 to 0.0546875
- low_down: bfloat16 [11008, 16], P('tp'), may hold values from -0.0546875 to 0.0546875
- high_down: bfloat16 [16, 4096], P(None, 'fsdp'), may hold values from -1.5 to 1.5
- norm_train: float32 [4096], P(('fsdp', 'tp')), may hold values from 0.25 to 1.75
- norm_step: float32 [4096], P(('fsdp', 'tp')), may hold values from -0.3 to 0.3
Outputs:
- serving_gate: bfloat16 [4096, 11008], P(None, 'tp')
- serving_up: bfloat16 [4096, 11008], P(None, 'tp')
- serving_down: bfloat16 [11008, 4096], P('tp')
- serve_norm: bfloat16 [4096], replicated
All inputs are finite; a program needn't handle non-finite values.
Results may differ from a plain program's by a relative error of at most 0.001.
Values may be sent and summed in bfloat16 or wider, within the bound.
A program may use at most 128 MiB of HBM per device.

v0:
```python
import jax
import jax.numpy as jnp
from jax import lax
from jax.sharding import Mesh
from jax.sharding import PartitionSpec as P

FSDP = ("fsdp_0", "fsdp_1")
FSDP_TP = ("fsdp_0", "fsdp_1", "tp_0", "tp_1")
TP = ("tp_0", "tp_1")
mix_rate = 2.0


def gather_turned(arrays, axis, dims):
    turned = [jnp.moveaxis(a, dim, 0) for a, dim in zip(arrays, dims)]
    widths = [t[0].size for t in turned]
    both = jnp.concatenate([t.reshape(-1, w) for t, w in zip(turned, widths)], axis=1)
    whole = lax.all_gather(both, axis, axis=0, tiled=True)
    parts = jnp.split(whole, [sum(widths[:k]) for k in range(1, len(widths))], axis=1)
    return tuple(
        (
            jnp.moveaxis(b.reshape(-1, *t.shape[1:]), 0, dim)
            for b, t, dim in zip(parts, turned, dims)
        )
    )


def laid_out(parts, dim):
    parts = jnp.moveaxis(parts, 0, dim)
    dims = parts.shape
    return parts.reshape(*dims[:dim], dims[dim] * dims[dim + 1], *dims[dim + 2 :])


def all_blocks(x, axes, sequence):
    parts = x[None]
    for k in sequence:
        parts = lax.all_gather(parts, axes[k], axis=0, tiled=True)
    held = [lax.axis_size(axes[k]) for k in reversed(sequence)]
    parts = parts.reshape(*held, *x.shape)
    turned = sorted(range(len(sequence)), key=lambda place: sequence[len(sequence) - 1 - place])
    return parts.transpose(*turned, *range(len(sequence), parts.ndim)).reshape(-1, *x.shape)


def gathered_by_axis(x, axes, sequence, dim):
    return laid_out(all_blocks(x, axes, sequence), dim)


def local(
    w_gate,
    low_gate,
    high_gate,
    w_up,
    low_up,
    high_up,
    w_down,
    low_down,
    high_down,
    norm_train,
    norm_step,
):
    whole_gate = w_gate.astype(jnp.float32) + mix_rate * jnp.dot(
        low_gate, high_gate, preferred_element_type=jnp.float32
    )
    whole_up = w_up.astype(jnp.float32) + mix_rate * jnp.dot(
        low_up, high_up, preferred_element_type=jnp.float32
    )
    whole_down = w_down.astype(jnp.float32) + mix_rate * jnp.dot(
        low_down, high_down, preferred_element_type=jnp.float32
    )
    narrow_gate, narrow_up, narrow_down = (
        whole_gate.astype(jnp.bfloat16),
        whole_up.astype(jnp.bfloat16),
        whole_down.astype(jnp.bfloat16),
    )
    serving_gate, serving_up, serving_down = gather_turned(
        (narrow_gate, narrow_up, narrow_down), FSDP, (0, 0, 1)
    )
    serve_norm = gathered_by_axis(
        (norm_train + norm_step).astype(jnp.bfloat16), FSDP_TP, (0, 2, 3, 1), 0
    )
    return (serving_gate, serving_up, serving_down, serve_norm)


def solution(mesh):
    finer = Mesh(mesh.devices.reshape(8, 2, 4, 4), ("fsdp_0", "fsdp_1", "tp_0", "tp_1"))
    in_specs = (
        P(FSDP, TP),
        P(FSDP, None),
        P(None, TP),
        P(FSDP, TP),
        P(FSDP, None),
        P(None, TP),
        P(TP, FSDP),
        P(TP, None),
        P(None, FSDP),
        P(FSDP_TP),
        P(FSDP_TP),
    )
    out_specs = (P(None, TP), P(None, TP), P(TP, None), P())
    return jax.shard_map(local, mesh=finer, in_specs=in_specs, out_specs=out_specs, check_vma=False)
```

profile of v0, /device:TPU:1, one launch (start us, length us, event | category | flops | bytes accessed | tf_op | source)
XLA Modules:
  0.0 139.7 jit_solution(4759233117201555211)
XLA Ops:
  7.2 0.0 copy-start
  7.2 0.0 all-gather.4.cloned.1.call-start
  7.2 0.7 copy-done
  7.9 1.3 fusion.3
  9.2 1.3 fusion.4
  10.5 0.0 copy-start.3
  10.6 0.0 copy-start.1
  10.6 0.0 copy-start.2
  10.6 1.3 fusion.6
  11.9 1.0 pad_maximum_fusion
  12.9 0.0 all-gather.4.cloned.1.call-update
  13.0 0.0 copy-done.3
  13.0 0.6 dynamic-slice
  14.2 0.0 copy-done.1
  14.2 0.0 copy-done.2
  14.3 0.2 dynamic-update-slice
  14.5 17.3 %all-reduce = bf16[128]{0:T(256)(128)(2,1)S(1)} all-reduce(bf16[128]{0:T(256)(128)(2,1)S(1)} %dynamic-update-slice), channel_id=2, replica_groups=mesh['fsdp_0'=8,'fsdp_1'=2,'tp_0'=4,'tp_1'=4] {'fsdp_0'}, use_global_device_ids=true, to_apply=%add | all-reduce | flops 128 | bytes 512
  31.8 0.1 reshape.12
  31.9 9.7 %all_gather.17 = bf16[32,16]{1,0:T(8,128)(2,1)S(1)} all-gather(bf16[8,16]{1,0:T(8,128)(2,1)S(1)} %reshape.12), channel_id=1, replica_groups=mesh['fsdp_0'=8,'fsdp_1'=2,'tp_0'=4,'tp_1'=4] {'tp_0'}, dimensions={0}, use_global_device_ids=true | all-gather | bytes 1280 | tf_op jit(solution)/shard_map/all_gather | solution.py:36
  41.6 0.1 copy.16
  41.6 10.1 %all-gather.1 = bf16[4,32,16]{1,2,0:T(8,128)(2,1)S(1)} all-gather(bf16[1,32,16]{1,2,0:T(8,128)(2,1)S(1)} %copy.16), channel_id=1, replica_groups=mesh['fsdp_0'=8,'fsdp_1'=2,'tp_0'=4,'tp_1'=4] {'tp_1'}, dimensions={0}, use_global_device_ids=true | all-gather | bytes 5120 | tf_op jit(solution)/shard_map/all_gather | solution.py:36
  51.8 0.1 copy.17
  51.9 10.0 %all_gather.19 = bf16[256,16]{1,0:T(8,128)(2,1)S(1)} all-gather(bf16[128,16]{1,0:T(8,128)(2,1)S(1)} %bitcast.17), channel_id=1, replica_groups=mesh['fsdp_0'=8,'fsdp_1'=2,'tp_0'=4,'tp_1'=4] {'fsdp_1'}, dimensions={0}, use_global_device_ids=true | all-gather | bytes 12288 | tf_op jit(solution)/shard_map/all_gather | solution.py:36
  61.9 0.7 reshape_reshape.3
  62.6 57.0 %all-gather.4.cloned.1.call-done = bf16[4096,2064]{0,1:T(8,128)(2,1)} async-done(((bf16[256,2064]{0,1:T(8,128)(2,1)}), bf16[4096,2064]{0,1:T(8,128)(2,1)}) %all-gather.4.cloned.1.call-update) | async-done | bytes 16908304 | tf_op jit(solution)/shard_map/all_gather | solution.py:17
  119.6 13.3 %slice_bitcast_fusion = (bf16[688,4096]{1,0:T(8,128)(2,1)}, bf16[4096,688]{0,1:T(8,128)(2,1)}, bf16[4096,688]{0,1:T(8,128)(2,1)}) fusion(bf16[4096,2064]{0,1:T(8,128)(2,1)} %all-gather.4.cloned.1.call-done), kind=kLoop, calls=%fused_computation | loop fusion | bytes 33816576 | tf_op jit(solution)/shard_map/transpose | solution.py:21
  (3 shorter events, 0.0 us)
Async XLA Ops:
  7.2 0.7 copy-start
  7.2 112.4 %all-gather.4.cloned.1.call-start = ((), (), s32[]{:S(2)}) async-start(), calls=%async_computation | async-start | bytes 17965056 | tf_op jit(solution)/shard_map/all_gather | solution.py:17
  10.5 2.4 %copy-start.3 = (u32[256]{0:T(256)S(1)}, u32[256]{0:T(256)}, u32[]{:S(2)}) copy-start(u32[256]{0:T(256)} %constant.7) | copy-start | bytes 3076
  10.6 3.7 %copy-start.1 = (f32[16]{0:T(128)S(1)}, f32[16]{0:T(128)}, u32[]{:S(2)}) copy-start(f32[16]{0:T(128)} %param.20) | copy-start | bytes 196
  10.6 3.7 %copy-start.2 = (f32[16]{0:T(128)S(1)}, f32[16]{0:T(128)}, u32[]{:S(2)}) copy-start(f32[16]{0:T(128)} %param.21) | copy-start | bytes 196
Sparse Core Ops, SparseCore 0:
  13.1 106.4 all-gather.3
where the time goes:
time: 140 us
  waiting for transfers between devices  57 us (41%)
  blocking collectives  47.1 us (34%)
  local copies, waits for them, and re-layouts  15.8 us (11%)
  between operations  14.8 us (11%)
  matrix products  3.94 us (3%)
    all_gather x1, waiting for transfers between devices, gather_turned(): whole = lax.all_gather(both, axis, axis=0, tiled=True)  57 us
    all_gather x3, blocking collectives, all_blocks(): parts = lax.all_gather(parts, axes[k], axis=0, tiled=True)  29.8 us
    unnamed x1, blocking collectives  17.3 us
    transpose x1, local copies, waits for them, and re-layouts, gather_turned(): jnp.moveaxis(b.reshape(-1, *t.shape[1:]), 0, dim)  13.3 us
  transfers between devices with their start and end apart: 1, of which 1 were waited for; matrix products, arithmetic and copies ran while one was open for 1% of the time, Pallas kernels for 0%

commit v1 on v0

--- a/solution.py
+++ b/solution.py
@@ -14,7 +14,9 @@
     turned = [jnp.moveaxis(a, dim, 0) for a, dim in zip(arrays, dims)]
     widths = [t[0].size for t in turned]
     both = jnp.concatenate([t.reshape(-1, w) for t, w in zip(turned, widths)], axis=1)
-    whole = lax.all_gather(both, axis, axis=0, tiled=True)
+    whole = jnp.concatenate(
+        lax.all_to_all(jnp.stack([both] * lax.axis_size(axis)), axis, 0, 0), axis=0
+    )
     parts = jnp.split(whole, [sum(widths[:k]) for k in range(1, len(widths))], axis=1)
     return tuple(
         (

time: 140 us -> 440 us (3.14)
  blocking collectives: 47.1 us -> 400 us
  waiting for transfers between devices: 57 us -> 0.01 us
  between operations: 14.8 us -> 1.38 us
  starting transfers between devices: 0.04 us -> 10.1 us
  local copies, waits for them, and re-layouts: 15.8 us -> 24 us
    unnamed x1, blocking collectives: 17.3 us -> 372 us
    all_gather x1 -> x0, waiting for transfers between devices: 57 us -> none  [gather_turned(): whole = lax.all_gather(both, axis, axis=0, tiled=True)]
    all_to_all x0 -> x1, starting transfers between devices: none -> 10.1 us  [gather_turned(): lax.all_to_all(jnp.stack([both] * lax.axis_size(axis)), axis, 0, 0)]
    reshape x0 -> x1, local copies, waits for them, and re-layouts: none -> 8.67 us  [gather_turned(): jnp.concatenate(lax.all_to_all(jnp.stack([both] * lax.axis_size(axis)), a...]
    transpose x1, local copies, waits for them, and re-layouts: 13.3 us -> 6.61 us  [gather_turned(): jnp.moveaxis(b.reshape(-1, *t.shape[1:]), 0, dim)]
    another operation x0 -> x1, local copies, waits for them, and re-layouts: none -> 6.16 us  [gather_turned(): jnp.stack([both] * lax.axis_size(axis))]
  transfers between devices with their start and end apart: 1 -> 1, of which waited for: 1 -> 0; matrix products, arithmetic and copies ran while one was open for 1% -> 0% of each run, Pallas kernels for 0% -> 0%
where the time goes in v1:
time: 440 us
  blocking collectives  400 us (91%)
  local copies, waits for them, and re-layouts  24 us (5%)
  starting transfers between devices  10.1 us (2%)
    unnamed x1, blocking collectives  372 us
    all_gather x3, blocking collectives, all_blocks(): parts = lax.all_gather(parts, axes[k], axis=0, tiled=True)  28.5 us
    all_to_all x1, starting transfers between devices, gather_turned(): lax.all_to_all(jnp.stack([both] * lax.axis_size(axis)), axis, 0, 0)  10.1 us
  transfers between devices with their start and end apart: 1, of which 0 were waited for; matrix products, arithmetic and copies ran while one was open for 0% of the time, Pallas kernels for 0%

profile of v1, /device:TPU:1, one launch (start us, length us, event | category | flops | bytes accessed | tf_op | source)
XLA Modules:
  0.0 439.9 jit_solution(18135587386448445910)
XLA Ops:
  0.6 0.0 copy-start
  0.6 0.7 copy-done
  1.4 1.3 fusion.3
  2.7 1.3 fusion.4
  4.0 1.3 fusion.6
  5.3 0.1 pad_maximum_fusion
  5.4 6.2 %stack.2 = bf16[16,256,2064]{1,2,0:T(8,128)(2,1)} broadcast(bf16[256,2064]{0,1:T(8,128)(2,1)S(1)} %pad_maximum_fusion), dimensions={1,2} | broadcast | bytes 17965056 | tf_op jit(solution)/shard_map/stack | solution.py:18
  11.6 0.0 copy-start.4
  11.6 0.0 copy-start.2
  11.6 0.0 copy-start.3
  11.6 10.1 %all-to-all-start = ((bf16[16,256,2064]{1,2,0:T(8,128)(2,1)}), bf16[16,256,2064]{1,2,0:T(8,128)(2,1)}, u32[]{:S(2)}, u32[]{:S(2)}) async-start(bf16[16,256,2064]{1,2,0:T(8,128)(2,1)} %stack.2), calls=%async_computation | async-start | bytes 33816576 | tf_op jit(solution)/shard_map/all_to_all | solution.py:18
  21.7 0.0 copy-done.4
  21.7 0.6 dynamic-slice
  22.9 0.0 copy-done.2
  22.9 0.0 copy-done.3
  23.0 0.2 dynamic-update-slice
  23.2 371.9 %all-reduce = bf16[128]{0:T(256)(128)(2,1)S(1)} all-reduce(bf16[128]{0:T(256)(128)(2,1)S(1)} %dynamic-update-slice), channel_id=2, replica_groups=mesh['fsdp_0'=8,'fsdp_1'=2,'tp_0'=4,'tp_1'=4] {'fsdp_0'}, use_global_device_ids=true, to_apply=%add | all-reduce | flops 128 | bytes 512
  395.1 0.1 reshape.18
  395.2 8.7 %all_gather.13 = bf16[32,16]{1,0:T(8,128)(2,1)S(1)} all-gather(bf16[8,16]{1,0:T(8,128)(2,1)S(1)} %reshape.18), channel_id=1, replica_groups=mesh['fsdp_0'=8,'fsdp_1'=2,'tp_0'=4,'tp_1'=4] {'tp_0'}, dimensions={0}, use_global_device_ids=true | all-gather | bytes 1280 | tf_op jit(solution)/shard_map/all_gather | solution.py:38
  403.8 0.1 copy.20
  403.9 9.5 %all-gather.1 = bf16[4,32,16]{1,2,0:T(8,128)(2,1)S(1)} all-gather(bf16[1,32,16]{1,2,0:T(8,128)(2,1)S(1)} %copy.20), channel_id=1, replica_groups=mesh['fsdp_0'=8,'fsdp_1'=2,'tp_0'=4,'tp_1'=4] {'tp_1'}, dimensions={0}, use_global_device_ids=true | all-gather | bytes 5120 | tf_op jit(solution)/shard_map/all_gather | solution.py:38
  413.4 0.1 copy.21
  413.5 10.3 %all_gather.15 = bf16[256,16]{1,0:T(8,128)(2,1)S(1)} all-gather(bf16[128,16]{1,0:T(8,128)(2,1)S(1)} %bitcast.20), channel_id=1, replica_groups=mesh['fsdp_0'=8,'fsdp_1'=2,'tp_0'=4,'tp_1'=4] {'fsdp_1'}, dimensions={0}, use_global_device_ids=true | all-gather | bytes 12288 | tf_op jit(solution)/shard_map/all_gather | solution.py:38
  423.9 0.7 reshape_reshape.3
  424.6 0.0 all-to-all-done
  424.6 8.7 %copy.23 = bf16[16,258,8,256]{3,2,0,1:T(8,128)(2,1)S(1)} copy(bf16[16,258,8,256]{3,2,1,0:T(8,128)(2,1)} %bitcast.8) | data formatting | bytes 33816576 | tf_op jit(solution)/shard_map/reshape | solution.py:17
  433.3 0.0 copy-start.1
  433.3 6.6 %slice_bitcast_fusion = (bf16[688,4096]{1,0:T(8,128)(2,1)}, bf16[4096,688]{0,1:T(8,128)(2,1)}, bf16[4096,688]{0,1:T(8,128)(2,1)}) fusion(bf16[4096,2064]{0,1:T(8,128)(2,1)S(1)} %bitcast.18), kind=kLoop, calls=%fused_computation | loop fusion | bytes 33816576 | tf_op jit(solution)/shard_map/transpose | solution.py:23
  439.9 0.0 copy-done.1
  (3 shorter events, 0.0 us)
Async XLA Ops:
  0.6 0.7 copy-start
  11.6 10.1 %copy-start.4 = (u32[256]{0:T(256)S(1)}, u32[256]{0:T(256)}, u32[]{:S(2)}) copy-start(u32[256]{0:T(256)} %constant.7) | copy-start | bytes 3076
  11.6 11.4 %copy-start.2 = (f32[16]{0:T(128)S(1)}, f32[16]{0:T(128)}, u32[]{:S(2)}) copy-start(f32[16]{0:T(128)} %param.20) | copy-start | bytes 196
  11.6 11.4 %copy-start.3 = (f32[16]{0:T(128)S(1)}, f32[16]{0:T(128)}, u32[]{:S(2)}) copy-start(f32[16]{0:T(128)} %param.21) | copy-start | bytes 196
  11.6 413.0 %all-to-all-start = ((bf16[16,256,2064]{1,2,0:T(8,128)(2,1)}), bf16[16,256,2064]{1,2,0:T(8,128)(2,1)}, u32[]{:S(2)}, u32[]{:S(2)}) async-start(bf16[16,256,2064]{1,2,0:T(8,128)(2,1)} %stack.2), calls=%async_computation | async-start | bytes 33816576 | tf_op jit(solution)/shard_map/all_to_all | solution.py:18
  433.3 6.6 %copy-start.1 = (bf16[16,688]{1,0:T(8,128)(2,1)S(1)}, bf16[16,688]{1,0:T(8,128)(2,1)}, u32[]{:S(2)}) copy-start(bf16[16,688]{1,0:T(8,128)(2,1)} %param.13) | copy-start | bytes 66052

commit v2 on v0

--- a/solution.py
+++ b/solution.py
@@ -33,7 +33,9 @@
 def all_blocks(x, axes, sequence):
     parts = x[None]
     for k in sequence:
-        parts = lax.all_gather(parts, axes[k], axis=0, tiled=True)
+        parts = jnp.concatenate(
+            lax.all_to_all(jnp.stack([parts] * lax.axis_size(axes[k])), axes[k], 0, 0), axis=0
+        )
     held = [lax.axis_size(axes[k]) for k in reversed(sequence)]
     parts = parts.reshape(*held, *x.shape)
     turned = sorted(range(len(sequence)), key=lambda place: sequence[len(sequence) - 1 - place])

time: 140 us -> 140 us (level)
  waiting for transfers between devices: 57 us -> 65.5 us
  blocking collectives: 47.1 us -> 39.8 us
    all_to_all x0 -> x4, blocking collectives: none -> 39.8 us  [all_blocks(): lax.all_to_all(jnp.stack([parts] * lax.axis_size(axes[k])), axes[k], 0, 0)]
    all_gather x3 -> x0, blocking collectives: 29.8 us -> none  [all_blocks(): parts = lax.all_gather(parts, axes[k], axis=0, tiled=True)]
    unnamed x1 -> x0, blocking collectives: 17.3 us -> none
    all_gather x1, waiting for transfers between devices: 57 us -> 65.5 us  [gather_turned(): whole = lax.all_gather(both, axis, axis=0, tiled=True)]
where the time goes in v2:
time: 140 us
  waiting for transfers between devices  65.5 us (47%)
  blocking collectives  39.8 us (28%)
  local copies, waits for them, and re-layouts  15.2 us (11%)
  between operations  14.1 us (10%)
  matrix products  3.94 us (3%)
    all_gather x1, waiting for transfers between devices, gather_turned(): whole = lax.all_gather(both, axis, axis=0, tiled=True)  65.5 us
    all_to_all x4, blocking collectives, all_blocks(): lax.all_to_all(jnp.stack([parts] * lax.axis_size(axes[k])), axes[k], 0, 0)  39.8 us
    transpose x1, local copies, waits for them, and re-layouts, gather_turned(): jnp.moveaxis(b.reshape(-1, *t.shape[1:]), 0, dim)  13.3 us
  transfers between devices with their start and end apart: 1, of which 1 were waited for; matrix products, arithmetic and copies ran while one was open for 1% of the time, Pallas kernels for 0%

profile of v2, /device:TPU:1, one launch (start us, length us, event | category | flops | bytes accessed | tf_op | source)
XLA Modules:
  0.0 139.7 jit_solution(12873930409085171200)
XLA Ops:
  7.2 0.0 copy-start
  7.2 0.0 all-gather.2.cloned.1.call-start
  7.2 0.7 copy-done
  7.9 1.3 fusion.3
  9.2 1.3 fusion.4
  10.5 0.0 copy-start.1
  10.6 0.0 copy-start.2
  10.6 1.3 fusion.6
  11.9 1.0 pad_maximum_fusion
  12.9 0.0 all-gather.2.cloned.1.call-update
  13.0 0.0 copy-done.1
  13.0 0.0 copy-done.2
  13.0 15.4 %all_to_all.20 = bf16[8,1,16]{2,1,0:T(2,128)(2,1)S(1)} all-to-all(bf16[8,1,16]{2,1,0:T(2,128)(2,1)S(1)} %stack.12), channel_id=1, replica_groups=mesh['fsdp_0'=8,'fsdp_1'=2,'tp_0'=4,'tp_1'=4] {'fsdp_0'}, dimensions={0} | all-to-all | bytes 512 | tf_op jit(solution)/shard_map/all_to_all | solution.py:37
  28.4 8.2 %all_to_all.21 = bf16[4,8,16]{2,1,0:T(8,128)(2,1)S(1)} all-to-all(bf16[4,8,16]{2,1,0:T(8,128)(2,1)S(1)} %stack.13), channel_id=1, replica_groups=mesh['fsdp_0'=8,'fsdp_1'=2,'tp_0'=4,'tp_1'=4] {'tp_0'}, dimensions={0} | all-to-all | bytes 2048 | tf_op jit(solution)/shard_map/all_to_all | solution.py:37
  36.6 0.1 copy.19
  36.7 0.1 reshape.14
  36.8 8.0 %all_to_all.22 = bf16[4,2,256]{2,1,0:T(2,128)(2,1)S(1)} all-to-all(bf16[4,2,256]{2,1,0:T(2,128)(2,1)S(1)} %reshape.14), channel_id=1, replica_groups=mesh['fsdp_0'=8,'fsdp_1'=2,'tp_0'=4,'tp_1'=4] {'tp_1'}, dimensions={0} | all-to-all | bytes 8192 | tf_op jit(solution)/shard_map/all_to_all | solution.py:37
  44.7 0.1 reshape.15
  44.8 0.1 stack_reshape.8
  44.9 8.2 %all_to_all.23 = bf16[2,128,16]{1,2,0:T(8,128)(2,1)S(1)} all-to-all(bf16[2,128,16]{1,2,0:T(8,128)(2,1)S(1)} %pad_maximum_fusion.1), channel_id=1, replica_groups=mesh['fsdp_0'=8,'fsdp_1'=2,'tp_0'=4,'tp_1'=4] {'fsdp_1'}, dimensions={0} | all-to-all | bytes 16384 | tf_op jit(solution)/shard_map/all_to_all | solution.py:37
  53.2 0.1 copy.21
  53.3 0.7 reshape_reshape.7
  54.0 65.5 %all-gather.2.cloned.1.call-done = bf16[4096,2064]{0,1:T(8,128)(2,1)} async-done(((bf16[256,2064]{0,1:T(8,128)(2,1)}), bf16[4096,2064]{0,1:T(8,128)(2,1)}) %all-gather.2.cloned.1.call-update) | async-done | bytes 16908304 | tf_op jit(solution)/shard_map/all_gather | solution.py:17
  119.5 13.3 %slice_bitcast_fusion = (bf16[688,4096]{1,0:T(8,128)(2,1)}, bf16[4096,688]{0,1:T(8,128)(2,1)}, bf16[4096,688]{0,1:T(8,128)(2,1)}) fusion(bf16[4096,2064]{0,1:T(8,128)(2,1)} %all-gather.2.cloned.1.call-done), kind=kLoop, calls=%fused_computation | loop fusion | bytes 33816576 | tf_op jit(solution)/shard_map/transpose | solution.py:21
  (8 shorter events, 0.1 us)
Async XLA Ops:
  7.2 0.7 copy-start
  7.2 112.4 %all-gather.2.cloned.1.call-start = ((), (), s32[]{:S(2)}) async-start(), calls=%async_computation.4 | async-start | bytes 17965056 | tf_op jit(solution)/shard_map/all_gather | solution.py:17
  10.5 2.4 %copy-start.1 = (f32[16]{0:T(128)S(1)}, f32[16]{0:T(128)}, u32[]{:S(2)}) copy-start(f32[16]{0:T(128)} %param.20) | copy-start | bytes 196
  10.6 2.4 %copy-start.2 = (f32[16]{0:T(128)S(1)}, f32[16]{0:T(128)}, u32[]{:S(2)}) copy-start(f32[16]{0:T(128)} %param.21) | copy-start | bytes 196
Sparse Core Ops, SparseCore 0:
  13.1 106.4 all-gather.1
